TPU v7x, 8 devices: a whole 2x2x1 slice. The times are simulated.
8 devices in a mesh: prompts: 1 (over z), model: 2 (over y), resp: 4 (over x, core).
Axes of the slice: x: 2, y: 2, z: 1, core: 2. Of those that a mesh axis runs over, the one named last changes fastest.
Arguments:
- x_prompt: bfloat16 [256, 896], P(('prompts', 'resp'))
- x_resp: bfloat16 [4, 256, 896], P(('prompts', 'resp'))
- targets: int32 [4, 256], P(('prompts', 'resp'))
- attn_norm: float32 [2, 896], replicated
- mlp_norm: float32 [2, 896], replicated
- w_q: bfloat16 [2, 896, 14, 64], P(None, None, 'model')
- w_k: bfloat16 [2, 896, 2, 64], P(None, None, 'model')
- w_v: bfloat16 [2, 896, 2, 64], P(None, None, 'model')
- w_o: bfloat16 [2, 14, 64, 896], P(None, 'model')
- w_gate: bfloat16 [2, 896, 4864], P(None, None, 'model')
- w_up: bfloat16 [2, 896, 4864], P(None, None, 'model')
- w_down: bfloat16 [2, 4864, 896], P(None, 'model')
- final_norm: float32 [896], replicated
- w_head: bfloat16 [896, 4096], P(None, 'model')
Outputs:
- output: float32 [4, 256], P(('prompts', 'resp'))
All inputs are finite; a program needn't handle non-finite values.
Results may differ from a plain program's by a relative error of at most 0.00312084.
Values are sent between devices in bfloat16 or wider.
A program may use at most 1 GiB of HBM per device.

v0:
```python
import math
import jax
import jax.numpy as jnp
from jax import lax
from jax.sharding import PartitionSpec as P

RMS_EPS = 1e-6
ROPE_BASE = 10000.0
NEG_BIG = -1e30


def rms_norm(x_in, norm_gain):
    x_f = x_in.astype(jnp.float32)
    mean_sq = jnp.mean(x_f * x_f, axis=-1, keepdims=True)
    return (x_f * lax.rsqrt(mean_sq + RMS_EPS) * norm_gain).astype(jnp.bfloat16)


def rope_tables(positions, head_dim):
    inv_freq = jnp.exp(jnp.arange(0, head_dim, 2, dtype=jnp.float32) * (-math.log(ROPE_BASE) / head_dim))
    angles = positions.astype(jnp.float32)[:, None] * inv_freq[None, :]
    return jnp.cos(angles), jnp.sin(angles)


def apply_rope(proj_f, cos_tab, sin_tab):
    half_dim = proj_f.shape[-1] // 2
    lo_half = proj_f[..., :half_dim]
    hi_half = proj_f[..., half_dim:]
    cos_b = cos_tab[:, None, :]
    sin_b = sin_tab[:, None, :]
    return jnp.concatenate([lo_half * cos_b - hi_half * sin_b, hi_half * cos_b + lo_half * sin_b], axis=-1)


def heads_proj(hidden, w_mat):
    return jnp.einsum('td,dhe->the', hidden, w_mat, preferred_element_type=jnp.float32)


def attend_local(queries, key_rows, val_rows, q_pos, k_pos):
    q_len, heads_loc, head_dim = queries.shape
    kv_loc = key_rows.shape[1]
    q_grp = queries.reshape(q_len, kv_loc, heads_loc // kv_loc, head_dim)
    scores = jnp.einsum('qhre,khe->hrqk', q_grp, key_rows, preferred_element_type=jnp.float32) * (1.0 / math.sqrt(head_dim))
    scores = jnp.where(k_pos[None, :] <= q_pos[:, None], scores, NEG_BIG)
    attn_probs = jax.nn.softmax(scores, axis=-1).astype(jnp.bfloat16)
    attn_mix = jnp.einsum('hrqk,khe->qhre', attn_probs, val_rows, preferred_element_type=jnp.float32)
    return attn_mix.astype(jnp.bfloat16).reshape(q_len, heads_loc, head_dim)


def finish_layer(x_in, attn_mix, w_out, gain_mlp, w_gate_l, w_up_l, w_down_l):
    attn_proj = lax.psum(jnp.einsum('the,hed->td', attn_mix, w_out, preferred_element_type=jnp.float32), 'model')
    x_mid = (x_in.astype(jnp.float32) + attn_proj).astype(jnp.bfloat16)
    hidden = rms_norm(x_mid, gain_mlp)
    gate_proj = jnp.dot(hidden, w_gate_l, preferred_element_type=jnp.float32)
    up_proj = jnp.dot(hidden, w_up_l, preferred_element_type=jnp.float32)
    act_vals = (jax.nn.silu(gate_proj) * up_proj).astype(jnp.bfloat16)
    down_proj = lax.psum(jnp.dot(act_vals, w_down_l, preferred_element_type=jnp.float32), 'model')
    return (x_mid.astype(jnp.float32) + down_proj).astype(jnp.bfloat16)


def token_logp(x_res, final_norm, w_head_loc, tgt_row, model_idx):
    logits = jnp.dot(rms_norm(x_res, final_norm), w_head_loc, preferred_element_type=jnp.float32)
    vocab_loc = logits.shape[1]
    top_val = lax.pmax(jnp.max(logits, axis=-1), 'model')
    exp_sum = jnp.sum(jnp.exp(logits - top_val[:, None]), axis=-1)
    vocab_ids = model_idx * vocab_loc + jnp.arange(vocab_loc)
    picked = jnp.sum(jnp.where(vocab_ids[None, :] == tgt_row[:, None], logits, 0.0), axis=-1)
    totals = lax.psum(jnp.stack([exp_sum, picked]), 'model')
    return totals[1] - top_val - jnp.log(totals[0])


def solution(mesh):
    group_size = mesh.shape['resp']
    rows_spec = P(('prompts', 'resp'), None)
    in_specs = (rows_spec, P(('prompts', 'resp'), None, None), rows_spec, P(), P(),
                P(None, None, 'model', None), P(None, None, 'model', None), P(None, None, 'model', None),
                P(None, 'model', None, None), P(None, None, 'model'), P(None, None, 'model'),
                P(None, 'model', None), P(), P(None, 'model'))

    def local_pass(x_piece, x_own, tgt_own, attn_norm, mlp_norm, w_q, w_k, w_v, w_o, w_gate, w_up, w_down, final_norm, w_head):
        piece_len = x_piece.shape[0]
        resp_len = x_own.shape[1]
        head_dim = w_q.shape[3]
        prompt_len = piece_len * group_size
        dev_idx = lax.axis_index('resp')
        model_idx = lax.axis_index('model')
        piece_pos = dev_idx * piece_len + jnp.arange(piece_len)
        resp_pos = prompt_len + jnp.arange(resp_len)
        tok_pos = jnp.concatenate([piece_pos, resp_pos])
        key_pos = jnp.concatenate([jnp.arange(prompt_len), resp_pos])
        tok_cos, tok_sin = rope_tables(tok_pos, head_dim)
        x_tok = jnp.concatenate([x_piece, x_own[0]], axis=0)

        hidden = rms_norm(x_tok, attn_norm[0])
        q_tok = apply_rope(heads_proj(hidden, w_q[0]), tok_cos, tok_sin).astype(jnp.bfloat16)
        k_tok = apply_rope(heads_proj(hidden, w_k[0]), tok_cos, tok_sin).astype(jnp.bfloat16)
        v_tok = heads_proj(hidden, w_v[0]).astype(jnp.bfloat16)
        kv_prompt = lax.all_gather(jnp.stack([k_tok[:piece_len], v_tok[:piece_len]]), 'resp', axis=1, tiled=True)
        key_rows = jnp.concatenate([kv_prompt[0], k_tok[piece_len:]], axis=0)
        val_rows = jnp.concatenate([kv_prompt[1], v_tok[piece_len:]], axis=0)
        attn_mix = attend_local(q_tok, key_rows, val_rows, tok_pos, key_pos)
        x_tok = finish_layer(x_tok, attn_mix, w_o[0], mlp_norm[0], w_gate[0], w_up[0], w_down[0])

        hidden = rms_norm(x_tok, attn_norm[1])
        k_tok = apply_rope(heads_proj(hidden, w_k[1]), tok_cos, tok_sin).astype(jnp.bfloat16)
        v_tok = heads_proj(hidden, w_v[1]).astype(jnp.bfloat16)
        q_own = apply_rope(heads_proj(hidden[piece_len:], w_q[1]), tok_cos[piece_len:], tok_sin[piece_len:]).astype(jnp.bfloat16)
        kv_prompt = lax.all_gather(jnp.stack([k_tok[:piece_len], v_tok[:piece_len]]), 'resp', axis=1, tiled=True)
        key_rows = jnp.concatenate([kv_prompt[0], k_tok[piece_len:]], axis=0)
        val_rows = jnp.concatenate([kv_prompt[1], v_tok[piece_len:]], axis=0)
        attn_mix = attend_local(q_own, key_rows, val_rows, resp_pos, key_pos)
        x_res = finish_layer(x_tok[piece_len:], attn_mix, w_o[1], mlp_norm[1], w_gate[1], w_up[1], w_down[1])
        return token_logp(x_res, final_norm, w_head, tgt_own[0], model_idx)[None, :]

    return jax.shard_map(local_pass, mesh=mesh, in_specs=in_specs, out_specs=rows_spec, check_vma=False)
```

profile of v0, /device:TPU:0, one launch (start us, length us, event | category | flops | bytes accessed | tf_op | source)
XLA Modules:
  0.0 249.6 jit_solution(11907829924966209848)
XLA Ops:
  6.6 1.2 fusion.49
  7.8 1.4 slice_reduce_fusion.1
  9.3 1.5 convolution_convert_fusion.1
  10.8 0.7 slice_bitcast_fusion.1
  11.4 1.5 convolution_bitcast_fusion.3
  12.9 0.7 pad_add_fusion
  13.6 0.9 multiply_cosine_fusion
  14.5 0.3 fusion.143
  14.8 0.6 copy-done.10
  15.4 0.1 copy.16
  15.5 10.3 %all_gather.6 = bf16[2,256,1,64]{3,0,2,1:T(2,128)(2,1)S(1)} all-gather(bf16[2,64,1,64]{3,0,2,1:T(2,128)(2,1)S(1)} %copy.16), channel_id=1, replica_groups=mesh['prompts'=1,'model'=2,'resp'=4] {'resp'}, dimensions={1}, use_global_device_ids=true | all-gather | bytes 81920 | tf_op jit(solution)/shard_map/all_gather | solution.py:96
  25.8 0.8 fusion.180
  26.6 0.7 copy.25
  27.4 0.1 fusion.178
  27.6 0.5 copy-done.28
  28.0 1.6 fusion.172
  29.7 0.1 copy.24
  29.8 0.2 broadcast_compare_fusion
  30.0 0.1 subtract_convert_fusion
  30.1 1.0 fusion.27
  31.2 2.0 copy-done
  33.2 1.4 fusion.23
  34.7 5.4 %convolution_bitcast_fusion = f32[320,896]{1,0:T(8,128)} fusion(f32[7,320]{1,0:T(8,128)S(1)} %fusion.23, f32[7,320]{1,0:T(8,128)S(1)} %get-tuple-element.37, f32[512,320,7]{0,1,2:T(8,128)} %copy-done, pred[320,512]{1,0:T(8,128)(4,1)S(1)} %broadcast_compare_fusion, bf16[2,7,64,896]{3,2,1,0:T(8,128)(2,1)} %param.22, bf16[256,1,64]{0,2,1:T(8,128)(2,1)S(1)} %copy-done.17, ...), kind=kOutput, calls=%fused_computation.45 | convolution fusion | flops 409710592 | bytes 6784512 | tf_op jit(solution)/shard_map/the,hed->td/dot_general | solution.py:49
  40.1 0.0 all-reduce.5.cloned.1.call-update
  40.1 0.2 all-reduce.7.cloned.1.call-start
  40.4 36.3 %all-reduce.5.cloned.1.call-done = f32[320,896]{1,0:T(8,128)} async-done(((f32[320,896]{1,0:T(8,128)}), f32[320,896]{1,0:T(8,128)}) %all-reduce.5.cloned.1.call-update) | async-done | bytes 1146896 | tf_op jit(solution)/shard_map/psum | solution.py:49
  76.7 1.5 fusion.53
  78.3 5.9 %fusion.9 = f32[320,2432]{1,0:T(8,128)} fusion(bf16[2,896,2432]{2,1,0:T(8,128)(2,1)} %param.23, bf16[320,896]{1,0:T(8,128)(2,1)S(1)} %get-tuple-element.16, f32[896]{0:T(1024)S(1)} %get-tuple-element.8, f32[320]{0:T(512)S(1)} %add_rsqrt_fusion.1), kind=kOutput, calls=%fused_computation.13 | convolution fusion | flops 1395752960 | bytes 8049408 | tf_op jit(solution)/shard_map/dot_general | solution.py:52
  84.1 9.1 %fusion.6 = f32[320,896]{1,0:T(8,128)} fusion(bf16[2,2432,896]{2,1,0:T(8,128)(2,1)} %param.25, bf16[2,896,2432]{2,1,0:T(8,128)(2,1)} %param.24, f32[320,2432]{1,0:T(8,128)} %fusion.9, bf16[320,896]{1,0:T(8,128)(2,1)S(1)} %get-tuple-element.16, f32[896]{0:T(1024)S(1)} %get-tuple-element.8, f32[320]{0:T(512)S(1)} %add_rsqrt_fusion.1), kind=kOutput, calls=%fused_computation.10 | convolution fusion | flops 2795028480 | bytes 13554432 | tf_op jit(solution)/shard_map/dot_general | solution.py:55
  93.2 0.0 all-reduce.9.cloned.1.call-start
  93.3 0.1 slice.203
  93.4 0.1 slice.205
  93.4 0.1 broadcast_compare_fusion.1
  93.6 36.2 %all-reduce.7.cloned.1.call-done = f32[320,896]{1,0:T(8,128)} async-done(((f32[320,896]{1,0:T(8,128)}), f32[320,896]{1,0:T(8,128)}) %all-reduce.7.cloned.1.call-update) | async-done | bytes 1146896 | tf_op jit(solution)/shard_map/psum | solution.py:55
  129.8 1.5 fusion.46
  131.3 0.2 fusion.48
  131.6 0.3 convolution_bitcast_fusion.2
  131.9 0.3 convolution_convert_fusion
  132.2 0.1 slice_bitcast_fusion
  132.3 0.3 fusion.147
  132.6 0.1 copy.19
  132.7 8.4 %all_gather.7 = bf16[2,256,1,64]{3,0,2,1:T(2,128)(2,1)S(1)} all-gather(bf16[2,64,1,64]{3,0,2,1:T(2,128)(2,1)S(1)} %copy.19), channel_id=1, replica_groups=mesh['prompts'=1,'model'=2,'resp'=4] {'resp'}, dimensions={1}, use_global_device_ids=true | all-gather | bytes 81920 | tf_op jit(solution)/shard_map/all_gather | solution.py:106
  141.1 0.2 fusion.179
  141.3 0.1 copy.27
  141.4 0.4 fusion.78
  141.8 0.1 copy.26
  141.9 0.1 subtract_convert_fusion.1
  142.0 0.8 fusion.29
  142.8 1.8 copy-done.1
  144.6 0.8 fusion.28
  145.4 0.0 copy-done.32
  145.4 4.4 %convolution_bitcast_fusion.1 = f32[256,896]{1,0:T(8,128)} fusion(bf16[2,7,64,896]{3,2,1,0:T(8,128)(2,1)S(1)} %copy-done.32, f32[7,256]{1,0:T(8,128)S(1)} %fusion.28, f32[7,256]{1,0:T(8,128)S(1)} %get-tuple-element.39, f32[512,256,7]{1,0,2:T(8,128)} %copy-done.1, pred[256,512]{0,1:T(8,128)(4,1)S(1)} %broadcast_compare_fusion.1, ...), kind=kOutput, calls=%fused_computation.49 | convolution fusion | flops 327794688 | bytes 5603328 | tf_op jit(solution)/shard_map/the,hed->td/dot_general | solution.py:49
  149.8 0.3 all-reduce.11.cloned.1.call-start
  150.1 30.4 %all-reduce.9.cloned.1.call-done = f32[256,896]{1,0:T(8,128)} async-done(((f32[256,896]{1,0:T(8,128)}), f32[256,896]{1,0:T(8,128)}) %all-reduce.9.cloned.1.call-update) | async-done | bytes 917520 | tf_op jit(solution)/shard_map/psum | solution.py:49
  180.4 1.4 fusion.60
  181.9 5.3 %fusion.4 = f32[256,2432]{1,0:T(8,128)} fusion(bf16[2,896,2432]{2,1,0:T(8,128)(2,1)} %param.23, bf16[256,896]{1,0:T(8,128)(2,1)S(1)} %get-tuple-element.12, f32[896]{0:T(1024)S(1)} %get-tuple-element.7, f32[256]{0:T(256)S(1)} %add_rsqrt_fusion.4), kind=kOutput, calls=%fused_computation.8 | convolution fusion | flops 1116602368 | bytes 7311872 | tf_op jit(solution)/shard_map/dot_general | solution.py:52
  187.2 8.1 %fusion = f32[256,896]{1,0:T(8,128)} fusion(bf16[2,2432,896]{2,1,0:T(8,128)(2,1)} %param.25, bf16[2,896,2432]{2,1,0:T(8,128)(2,1)} %param.24, f32[256,2432]{1,0:T(8,128)} %fusion.4, bf16[256,896]{1,0:T(8,128)(2,1)S(1)} %get-tuple-element.12, f32[896]{0:T(1024)S(1)} %get-tuple-element.7, f32[256]{0:T(256)S(1)} %add_rsqrt_fusion.4), kind=kOutput, calls=%fused_computation.4 | convolution fusion | flops 2236022784 | bytes 12587520 | tf_op jit(solution)/shard_map/dot_general | solution.py:55
  195.3 31.6 %all-reduce.11.cloned.1.call-done = f32[256,896]{1,0:T(8,128)} async-done(((f32[256,896]{1,0:T(8,128)}), f32[256,896]{1,0:T(8,128)}) %all-reduce.11.cloned.1.call-update) | async-done | bytes 917520 | tf_op jit(solution)/shard_map/psum | solution.py:55
  226.9 1.4 fusion.57
  228.3 3.7 %fusion.182 = (f32[256]{0:T(256)S(1)}, f32[256,2048]{1,0:T(8,128)S(1)}) fusion(bf16[896,2048]{1,0:T(8,128)(2,1)} %param.27, f32[896]{0:T(1024)S(1)} %copy-done.26, f32[256]{0:T(256)S(1)} %add_rsqrt_fusion.3, f32[256,896]{1,0:T(8,128)} %all-reduce.11.cloned.1.call-done, bf16[256,896]{1,0:T(8,128)(2,1)S(1)} %get-tuple-element.12), kind=kOutput, calls=%fused_computation.202 | convolution fusion | flops 941653760 | bytes 7149056 | tf_op jit(solution)/shard_map/dot_general | solution.py:60
  232.0 4.9 %pmax.7 = f32[256]{0:T(256)S(1)} all-reduce(f32[256]{0:T(256)S(1)} %get-tuple-element.41), channel_id=1, replica_groups=mesh['prompts'=1,'model'=2,'resp'=4] {'model'}, use_global_device_ids=true, to_apply=%region_14.15 | all-reduce | flops 256 | bytes 2048 | tf_op jit(solution)/shard_map/pmax | solution.py:62
  237.0 0.6 exponential_reduce_fusion
  237.6 4.9 %psum.39 = f32[2,256]{1,0:T(2,128)S(1)} all-reduce(f32[2,256]{1,0:T(2,128)S(1)} %pad_maximum_fusion.3), channel_id=1, replica_groups=mesh['prompts'=1,'model'=2,'resp'=4] {'model'}, use_global_device_ids=true, to_apply=%region_17.18 | all-reduce | flops 512 | bytes 4096 | tf_op jit(solution)/shard_map/psum | solution.py:66
  242.5 0.6 subtract_subtract_fusion
  (85 shorter events, 0.3 us)
Async XLA Ops:
  6.5 70.2 %all-reduce.5.cloned.1.call-start = ((), (), s32[]{:S(2)}) async-start(), calls=%async_computation | async-start | bytes 2293760 | tf_op jit(solution)/shard_map/psum | solution.py:49
  6.5 7.1 %copy-start.19 = (s32[256]{0:T(256)}, s32[256]{0:T(256)S(1)}, u32[]{:S(2)}) copy-start(s32[256]{0:T(256)S(1)} %iota_add_fusion.1) | copy-start | bytes 3076
  6.6 9.0 %copy-start.24 = (f32[32]{0:T(128)}, f32[32]{0:T(128)S(1)}, u32[]{:S(2)}) copy-start(f32[32]{0:T(128)S(1)} %multiply_exponential_fusion) | copy-start | bytes 388
  7.8 19.5 %copy-start.3 = (bf16[2,896,7,64]{1,3,2,0:T(8,128)(2,1)S(1)}, bf16[2,896,7,64]{1,3,2,0:T(8,128)(2,1)}, u32[]{:S(2)}) copy-start(bf16[2,896,7,64]{1,3,2,0:T(8,128)(2,1)} %param.19) | copy-start | bytes 4816900
  7.8 5.8 %copy-start.29 = (f32[320]{0:T(512)}, f32[320]{0:T(512)S(1)}, u32[]{:S(2)}) copy-start(f32[320]{0:T(512)S(1)} %add_rsqrt_fusion.2) | copy-start | bytes 3844
  9.3 4.3 %copy-start.27 = (f32[896]{0:T(1024)}, f32[896]{0:T(1024)S(1)}, u32[]{:S(2)}) copy-start(f32[896]{0:T(1024)S(1)} %get-tuple-element.10) | copy-start | bytes 10756
  12.9 14.6 %copy-start.2 = (bf16[1,256,896]{2,1,0:T(8,128)(2,1)S(1)}, bf16[1,256,896]{2,1,0:T(8,128)(2,1)}, u32[]{:S(2)}) copy-start(bf16[1,256,896]{2,1,0:T(8,128)(2,1)} %param.15) | copy-start | bytes 1376260
  13.6 1.9 copy-start.14
  14.8 0.6 copy-start.10
  14.8 0.6 copy-start.8
  27.3 0.7 copy-start.28
  27.3 0.7 copy-start.30
  27.4 2.3 copy-start.20
  27.5 2.2 copy-start.4
  27.5 2.3 copy-start.22
  27.5 2.4 copy-start.6
  27.5 2.4 copy-start.7
  27.5 2.5 %copy-start.9 = (bf16[320,1,32]{0,2,1:T(8,128)(2,1)S(1)}, bf16[320,1,32]{0,2,1:T(8,128)(2,1)}, u32[]{:S(2)}) copy-start(bf16[320,1,32]{0,2,1:T(8,128)(2,1)} %copy-done.8) | copy-start | bytes 61444
  27.5 2.5 %copy-start.11 = (bf16[320,1,32]{0,2,1:T(8,128)(2,1)S(1)}, bf16[320,1,32]{0,2,1:T(8,128)(2,1)}, u32[]{:S(2)}) copy-start(bf16[320,1,32]{0,2,1:T(8,128)(2,1)} %copy-done.10) | copy-start | bytes 61444
  27.6 2.5 %copy-start.16 = (bf16[1,256,1,64]{1,3,2,0:T(8,128)(2,1)S(1)}, bf16[1,256,1,64]{1,3,2,0:T(8,128)(2,1)}, u32[]{:S(2)}) copy-start(bf16[1,256,1,64]{1,3,2,0:T(8,128)(2,1)} %copy.25) | copy-start | bytes 98308
  31.1 2.1 copy-start
  31.2 3.5 %copy-start.17 = (bf16[256,1,64]{0,2,1:T(8,128)(2,1)S(1)}, bf16[256,1,64]{0,2,1:T(8,128)(2,1)}, u32[]{:S(2)}) copy-start(bf16[256,1,64]{0,2,1:T(8,128)(2,1)} %slice_bitcast_fusion.1) | copy-start | bytes 98308
  34.6 5.7 %copy-start.23 = (f32[2,896]{1,0:T(2,128)S(1)}, f32[2,896]{1,0:T(2,128)}, u32[]{:S(2)}) copy-start(f32[2,896]{1,0:T(2,128)} %param.18) | copy-start | bytes 21508
  34.6 42.1 %copy-start.5 = (bf16[64,896]{1,0:T(8,128)(2,1)S(1)}, bf16[64,896]{1,0:T(8,128)(2,1)}, u32[]{:S(2)}) copy-start(bf16[64,896]{1,0:T(8,128)(2,1)} %param.14) | copy-start | bytes 344068
  40.1 89.7 %all-reduce.7.cloned.1.call-start = ((), (), s32[]{:S(2)}) async-start(), calls=%async_computation.1 | async-start | bytes 2293760 | tf_op jit(solution)/shard_map/psum | solution.py:55
  84.1 9.3 %copy-start.21 = (s32[256]{0:T(256)S(1)}, s32[256]{0:T(256)}, u32[]{:S(2)}) copy-start(s32[256]{0:T(256)} %copy-done.19) | copy-start | bytes 3076
  93.2 38.1 %copy-start.18 = (f32[896]{0:T(1024)S(1)}, f32[896]{0:T(1024)}, u32[]{:S(2)}) copy-start(f32[896]{0:T(1024)} %get-tuple-element.9) | copy-start | bytes 10756
  93.2 38.4 %copy-start.12 = (bf16[2,896,1,64]{1,3,2,0:T(8,128)(2,1)S(1)}, bf16[2,896,1,64]{1,3,2,0:T(8,128)(2,1)}, u32[]{:S(2)}) copy-start(bf16[2,896,1,64]{1,3,2,0:T(8,128)(2,1)} %param.20) | copy-start | bytes 688132
  93.2 38.6 %copy-start.13 = (bf16[2,896,1,64]{1,3,2,0:T(8,128)(2,1)S(1)}, bf16[2,896,1,64]{1,3,2,0:T(8,128)(2,1)}, u32[]{:S(2)}) copy-start(bf16[2,896,1,64]{1,3,2,0:T(8,128)(2,1)} %param.21) | copy-start | bytes 688132
  93.2 87.2 %all-reduce.9.cloned.1.call-start = ((), (), s32[]{:S(2)}) async-start(), calls=%async_computation.2 | async-start | bytes 1835008 | tf_op jit(solution)/shard_map/psum | solution.py:49
  93.6 38.7 %copy-start.15 = (f32[320]{0:T(512)S(1)}, f32[320]{0:T(512)}, u32[]{:S(2)}) copy-start(f32[320]{0:T(512)} %copy-done.14) | copy-start | bytes 3844
  93.6 38.7 %copy-start.25 = (f32[32]{0:T(128)S(1)}, f32[32]{0:T(128)}, u32[]{:S(2)}) copy-start(f32[32]{0:T(128)} %copy-done.24) | copy-start | bytes 388
  142.8 1.8 copy-start.1
  142.8 2.6 %copy-start.32 = (bf16[2,7,64,896]{3,2,1,0:T(8,128)(2,1)S(1)}, bf16[2,7,64,896]{3,2,1,0:T(8,128)(2,1)}, u32[]{:S(2)}) copy-start(bf16[2,7,64,896]{3,2,1,0:T(8,128)(2,1)} %param.22) | copy-start | bytes 4816900
  149.8 77.1 %all-reduce.11.cloned.1.call-start = ((), (), s32[]{:S(2)}) async-start(), calls=%async_computation.3 | async-start | bytes 1835008 | tf_op jit(solution)/shard_map/psum | solution.py:55
  187.1 41.1 %copy-start.26 = (f32[896]{0:T(1024)S(1)}, f32[896]{0:T(1024)}, u32[]{:S(2)}) copy-start(f32[896]{0:T(1024)} %param.26) | copy-start | bytes 10756
  228.3 8.7 %copy-start.31 = (s32[1,256]{1,0:T(1,128)S(1)}, s32[1,256]{1,0:T(1,128)}, u32[]{:S(2)}) copy-start(s32[1,256]{1,0:T(1,128)} %param.16) | copy-start | bytes 3076
Sparse Core Ops, SparseCore 0:
  40.2 36.4 all-reduce.4
  93.3 36.4 all-reduce.6
  149.9 30.4 all-reduce.8
  195.4 31.4 all-reduce.10
where the time goes:
time: 250 us
  waiting for transfers between devices  135 us (54%)
  matrix products  49.2 us (20%)
  blocking collectives  28.6 us (11%)
  between operations  13.7 us (5%)
  other arithmetic  13.3 us (5%)
  local copies, waits for them, and re-layouts  9.75 us (4%)
    psum x2, waiting for transfers between devices, finish_layer(): lax.psum(jnp.dot(act_vals, w_down_l, preferred_element_type=jnp.float32),...  67.7 us
    psum x2, waiting for transfers between devices, finish_layer(): lax.psum(jnp.einsum('the,hed->td', attn_mix, w_out, preferred_element_typ...  66.7 us
    all_gather x2, blocking collectives, local_pass(): lax.all_gather(jnp.stack([k_tok[:piece_len], v_tok[:piece_len]]), 'resp',...  18.7 us
    dot_general x2, matrix products, finish_layer(): jnp.dot(act_vals, w_down_l, preferred_element_type=jnp.float32)  17.2 us
    dot_general x2, matrix products, finish_layer(): gate_proj = jnp.dot(hidden, w_gate_l, preferred_element_type=jnp.float32)  11.2 us
    dot_general x2, matrix products, finish_layer(): jnp.einsum('the,hed->td', attn_mix, w_out, preferred_element_type=jnp.flo...  9.81 us
    reduce_sum x5, other arithmetic, rms_norm(): mean_sq = jnp.mean(x_f * x_f, axis=-1, keepdims=True)  7.06 us
    unnamed x70, local copies, waits for them, and re-layouts  6.01 us
  transfers between devices with their start and end apart: 4, of which 4 were waited for; matrix products, arithmetic and copies ran while one was open for 0% of the time, Pallas kernels for 0%

commit v1 on v0

v1 whole, which is shorter than its diff:
```python
import functools
import math

import jax
import jax.numpy as jnp
import numpy as np
from jax import lax
from jax.experimental import pallas as pl
from jax.experimental.pallas import tpu as pltpu
from jax.sharding import PartitionSpec as P

RMS_EPS = 1e-6
ROPE_BASE = 10000.0
NEG_BIG = -1e30
BF16 = jnp.bfloat16
F32 = jnp.float32

D = 896
HD = 64
PIECE = 64
RESP = 256
PROMPT = 256
ROWS = PIECE + RESP
FF = 2432
VOC = 2048
QROWS = 448
GROUP = 4
GAIN_PAD = 1024
CHUNKS = ((0, 64), (64, 128), (192, 128))
WO_QUARTER = QROWS // GROUP
WO_PIECES = ((0, 64), (64, 48))
FF_BLOCKS = ((0, 512), (512, 512), (1024, 512), (1536, 512), (2048, 384))


def rope_constants():
    inv = np.exp(np.arange(0, HD, 2, dtype=np.float32) * np.float32(-math.log(ROPE_BASE) / HD)).astype(np.float32)
    ang = np.arange(PROMPT + RESP, dtype=np.float32)[:, None] * inv[None, :]
    cos, sin = np.cos(ang).astype(np.float32), np.sin(ang).astype(np.float32)
    return np.concatenate([cos] * 4, axis=1), np.concatenate([-sin, sin] * 2, axis=1)


def mm(a, b):
    return jnp.dot(a, b, preferred_element_type=F32)


def mm_t(a, b):
    return lax.dot_general(a, b, (((1,), (1,)), ((), ())), preferred_element_type=F32)


def rms(x_f, gain):
    mean_sq = jnp.mean(x_f * x_f, axis=-1, keepdims=True)
    return (x_f * lax.rsqrt(mean_sq + RMS_EPS) * gain).astype(BF16)


def kernel(xp, xr, tgt, an, mn, wq, wk, wv, wo, wg, wu, wd, fn, wh, cs, sn, out,
           vx, vcs, vsn, vtgt, van, vmn, vfn, wqkv, womy, woot, vg, vu, vd, vh,
           kv, qb, amine, asnd, arcv, xm, ub, part, prcv, x1, hb, lgt, st_s, st_r,
           lsem, ssem, rsem):
    me = lax.axis_index('resp')
    side = lax.axis_index('model')
    other = 1 - side
    y_peer = {'model': other}
    d_peer = {'resp': me + 1 - 2 * lax.rem(me, 2)}
    x_peer = {'resp': lax.rem(me + 2, 4)}

    counts = {'l': 0, 'r': 0}

    def load(src, dst):
        cp = pltpu.make_async_copy(src, dst, lsem.at[counts['l']])
        counts['l'] += 1
        cp.start()
        return cp

    def remote(src, dst, peer):
        k = counts['r']
        counts['r'] += 1
        return pltpu.make_async_remote_copy(src_ref=src, dst_ref=dst, send_sem=ssem.at[k], recv_sem=rsem.at[k],
                                            device_id=peer, device_id_type=pl.DeviceIdType.MESH)

    sent = []

    def send(cp):
        cp.start()
        sent.append(cp)
        return cp

    def load_qkv(l):
        return [load(wq.at[l], wqkv.at[l, pl.ds(0, QROWS)]), load(wk.at[l], wqkv.at[l, pl.ds(QROWS, HD)]),
                load(wv.at[l], wqkv.at[l, pl.ds(QROWS + HD, HD)]), load(wv.at[l], wqkv.at[l, pl.ds(QROWS + 2 * HD, HD)])]

    first = [load(xp, vx.at[pl.ds(0, PIECE)]), load(an, van.at[:, pl.ds(0, D)])] + load_qkv(0)
    my_pos = pl.multiple_of(me * PIECE, PIECE)
    first += [load(cs.at[pl.ds(my_pos, PIECE)], vcs.at[pl.ds(0, PIECE)]), load(sn.at[pl.ds(my_pos, PIECE)], vsn.at[pl.ds(0, PIECE)])]
    second = [load(xr, vx.at[pl.ds(PIECE, RESP)]), load(cs.at[pl.ds(PROMPT, RESP)], vcs.at[pl.ds(PIECE, RESP)]),
              load(sn.at[pl.ds(PROMPT, RESP)], vsn.at[pl.ds(PIECE, RESP)])]

    barrier = pltpu.get_barrier_semaphore()
    pl.semaphore_signal(barrier, inc=1, device_id=y_peer, device_id_type=pl.DeviceIdType.MESH)
    for k in range(1, GROUP):
        pl.semaphore_signal(barrier, inc=1, device_id={'resp': lax.rem(me + k, GROUP)}, device_id_type=pl.DeviceIdType.MESH)
    pl.semaphore_wait(barrier, GROUP)

    def wo_slot(l, q, piece):
        start, size = WO_PIECES[piece]
        return woot.at[l, pl.ds(pl.multiple_of(q * WO_QUARTER + start, 16), size)]

    def wo_over_y(l):
        cps = []
        for start, size in WO_PIECES:
            rows = pl.ds(pl.multiple_of(me * WO_QUARTER + start, 16), size)
            cps.append(send(remote(wo.at[l, rows], woot.at[l, rows], y_peer)))
        return cps

    def wo_relay_own(l, piece, y_copy):
        y_copy.wait_recv()
        slot = wo_slot(l, me, piece)
        return send(remote(slot, slot, x_peer)), send(remote(slot, slot, d_peer))

    def wo_relay_x(l, piece, x_copy):
        x_copy.wait_recv()
        slot = wo_slot(l, lax.rem(me + 2, 4), piece)
        return send(remote(slot, slot, d_peer))

    wo_y0 = wo_over_y(0)

    zeros = jnp.zeros((512 - QROWS, D), BF16)
    for l in range(2):
        womy[l, QROWS:512] = zeros
        woot[l, QROWS:512] = zeros

    for cp in first:
        cp.wait()

    def halves(src, dst, l, rows):
        h = rows // 2
        return [load(src.at[l, pl.ds(0, h)], dst.at[l, pl.ds(0, h)]), load(src.at[l, pl.ds(h, h)], dst.at[l, pl.ds(h, h)])]

    lane = lax.broadcasted_iota(jnp.int32, (1, 128), 1)
    lo_head = lane < HD
    lo_half = lax.rem(lane, HD) < (HD // 2)

    def project(l, row0, n, hidden, kv_row):
        y = mm_t(hidden, wqkv[l])
        cos, sin = vcs[row0:row0 + n], vsn[row0:row0 + n]
        roped = []
        for j in range(4):
            b = y[:, 128 * j:128 * (j + 1)]
            partner = jnp.where(lo_half, pltpu.roll(b, 128 - HD // 2, 1), pltpu.roll(b, HD // 2, 1))
            roped.append(b * cos + partner * sin)
            qb[row0:row0 + n, 128 * j:128 * (j + 1)] = roped[-1].astype(BF16)
        kv[l, pl.ds(kv_row, n)] = jnp.where(lo_head, y[:, 512:640], roped[3]).astype(BF16)

    def share_kv(l):
        slot = kv.at[l, pl.ds(my_pos, PIECE)]
        return [send(remote(slot, slot, {'resp': lax.rem(me + k, GROUP)})) for k in range(1, GROUP)]

    def a_base(row0):
        return row0 * 7 // 2

    def attend(l, c, base, nk):
        row0, n = CHUNKS[c]
        kv_f = kv[l, 0:nk].astype(F32)
        kv_r = pltpu.roll(kv_f, HD, 1)
        k_even = jnp.where(lo_head, kv_r, 0.0).astype(BF16)
        k_odd = jnp.where(lo_head, 0.0, kv_f).astype(BF16)
        v_even = jnp.where(lo_head, kv_f, 0.0).astype(BF16)
        v_odd = jnp.where(lo_head, 0.0, kv_r).astype(BF16)
        q = [qb[row0:row0 + n, 128 * j:128 * (j + 1)] for j in range(4)]
        s_even = mm_t(jnp.concatenate(q, axis=0), k_even)
        s_odd = mm_t(jnp.concatenate(q[:3], axis=0), k_odd)
        vis = max(nk - n, 0) if c else 0
        keep = (lax.broadcasted_iota(jnp.int32, (n, nk - vis), 1) + vis) <= (base + lax.broadcasted_iota(jnp.int32, (n, nk - vis), 0))

        def probs(s):
            tail = jnp.where(keep, s[:, vis:], NEG_BIG)
            s = jnp.concatenate([s[:, :vis], tail], axis=1) if vis else tail
            top = jnp.max(s, axis=-1, keepdims=True)
            e = jnp.exp2((s - top) * (math.log2(math.e) / math.sqrt(HD)))
            return (e * (1.0 / jnp.sum(e, axis=-1, keepdims=True))).astype(BF16)

        p_even = jnp.concatenate([probs(s_even[j * n:(j + 1) * n]) for j in range(4)], axis=0)
        p_odd = jnp.concatenate([probs(s_odd[j * n:(j + 1) * n]) for j in range(3)], axis=0)
        o_even = mm(p_even, v_even)
        o_odd = mm(p_odd, v_odd)
        ab = a_base(row0)
        for j in range(3):
            blk = (o_even[j * n:(j + 1) * n] + o_odd[j * n:(j + 1) * n]).astype(BF16)
            amine[row0:row0 + n, 128 * j:128 * (j + 1)] = blk
            asnd[l, ab + j * n:ab + (j + 1) * n] = blk
        last = o_even[3 * n:4 * n]
        amine[row0:row0 + n, 384:512] = last.astype(BF16)
        asnd[l, ab + 3 * n:ab + 7 * n // 2] = (last[:n // 2] + pltpu.roll(last[n // 2:], HD, 1)).astype(BF16)
        rows = pl.ds(ab, 7 * n // 2)
        return send(remote(asnd.at[l, rows], arcv.at[l, rows], y_peer))

    def merge_attention(l, c, x_ref, a_copy):
        row0, n = CHUNKS[c]
        a_copy.wait_recv()
        ab = a_base(row0)
        packed = arcv[l, ab + 3 * n:ab + 7 * n // 2].astype(F32)
        last = jnp.concatenate([packed, pltpu.roll(packed, HD, 1)], axis=0).astype(BF16)
        a_oth = jnp.concatenate([arcv[l, ab + j * n:ab + (j + 1) * n] for j in range(3)] + [last], axis=1)
        proj = mm(amine[row0:row0 + n], womy[l]) + mm(a_oth, woot[l])
        xm[row0:row0 + n] = (x_ref[row0:row0 + n].astype(F32) + proj).astype(BF16)

    def mlp(l, c):
        row0, n = CHUNKS[c]
        g = rms(xm[row0:row0 + n].astype(F32), vmn[l:l + 1, 0:D])
        for b0, bn in FF_BLOCKS:
            gate = mm(g, vg[l, :, b0:b0 + bn])
            up = mm(g, vu[l, :, b0:b0 + bn])
            ub[0:n, b0:b0 + bn] = (gate * (1.0 / (1.0 + jnp.exp(-gate))) * up).astype(BF16)
        part[l, row0:row0 + n] = mm(ub[0:n], vd[l])
        h = n // 2
        src = part.at[l, pl.ds(pl.multiple_of(row0 + other * h, 16), h)]
        return send(remote(src, prcv.at[l, pl.ds(row0 // 2, h)], y_peer))

    def home_rows(c):
        row0, n = CHUNKS[c]
        return pl.ds(pl.multiple_of(row0 + side * (n // 2), 16), n // 2)

    def home_sum(l, c, p_copy):
        row0, n = CHUNKS[c]
        rows = home_rows(c)
        p_copy.wait_recv()
        total = part[l, rows] + prcv[l, row0 // 2:row0 // 2 + n // 2]
        return (xm[rows].astype(F32) + total).astype(BF16)

    def close_layer0(c, p_copy):
        rows = home_rows(c)
        x1[rows] = home_sum(0, c, p_copy)
        return send(remote(x1.at[rows], x1.at[rows], y_peer))

    def close_layer1(c, p_copy):
        rows = home_rows(c)
        hb[rows] = rms(home_sum(1, c, p_copy).astype(F32), vfn[:, 0:D])
        return send(remote(hb.at[rows], hb.at[rows], y_peer))

    def head(c, h_copy):
        row0, n = CHUNKS[c]
        t0 = row0 - PIECE
        h_copy.wait_recv()
        hidden = hb[row0:row0 + n]
        want = jnp.broadcast_to(vtgt[0:1, t0:t0 + n].astype(F32), (128, n)).T.astype(jnp.int32)[:, 0:1]
        top = None
        picked = None
        for b in range(4):
            lg = mm(hidden, vh[:, 512 * b:512 * (b + 1)])
            lgt[:, 512 * b:512 * (b + 1)] = lg
            ids = side * VOC + 512 * b + lax.broadcasted_iota(jnp.int32, (n, 512), 1)
            hit = jnp.where(ids == want, lg, 0.0)
            part_top = jnp.max(lg, axis=-1, keepdims=True)
            part_hit = jnp.sum(hit, axis=-1, keepdims=True)
            top = part_top if top is None else jnp.maximum(top, part_top)
            picked = part_hit if picked is None else picked + part_hit
        total = jnp.sum(jnp.exp(lgt[...] - top), axis=-1, keepdims=True)
        table = jnp.where(lane == 0, top, jnp.where(lane == 1, total, picked))
        st_s[c - 1] = table.T[0:8]
        return send(remote(st_s.at[c - 1], st_r.at[c - 1], y_peer))

    def finish(c, s_copy):
        row0, n = CHUNKS[c]
        s_copy.wait_recv()
        a, b = st_s[c - 1], st_r[c - 1]
        top = jnp.maximum(a[0:1], b[0:1])
        total = a[1:2] * jnp.exp(a[0:1] - top) + b[1:2] * jnp.exp(b[0:1] - top)
        out[0:1, row0 - PIECE:row0 - PIECE + n] = (a[2:3] + b[2:3]) - (top + jnp.log(total))

    hidden_p = rms(vx[0:PIECE].astype(F32), van[0:1, 0:D])
    project(0, 0, PIECE, hidden_p, my_pos)
    kv_cps = share_kv(0)
    for cp in second:
        cp.wait()
    w_my0 = [load(wo.at[0], womy.at[0, pl.ds(0, QROWS)]), load(mn, vmn.at[:, pl.ds(0, D)])]
    w_mlp0 = halves(wg, vg, 0, D) + halves(wu, vu, 0, D) + halves(wd, vd, 0, FF)
    project(0, PIECE, RESP, rms(vx[PIECE:ROWS].astype(F32), van[0:1, 0:D]), PROMPT)
    w_qkv1 = load_qkv(1)
    w_my1 = [load(wo.at[1], womy.at[1, pl.ds(0, QROWS)])]
    w_mlp1 = halves(wg, vg, 1, D) + halves(wu, vu, 1, D) + halves(wd, vd, 1, FF)
    w_head = [load(wh.at[pl.ds(0, D // 2)], vh.at[pl.ds(0, D // 2)]), load(wh.at[pl.ds(D // 2, D // 2)], vh.at[pl.ds(D // 2, D // 2)]),
              load(tgt, vtgt), load(fn, vfn.at[:, pl.ds(0, D)])]
    for cp in kv_cps:
        cp.wait_recv()
    a_cps = [attend(0, 0, my_pos, PROMPT), attend(0, 1, PROMPT, 384)]
    own0 = wo_relay_own(0, 0, wo_y0[0])
    a_cps.append(attend(0, 2, 384, 512))
    own1 = wo_relay_own(0, 1, wo_y0[1])
    d0 = wo_relay_x(0, 0, own0[0])
    wo_y1 = wo_over_y(1)
    d1 = wo_relay_x(0, 1, own1[0])
    for cp in w_my0 + w_mlp0:
        cp.wait()
    for cp in (own0[1], own1[1], d0, d1):
        cp.wait_recv()

    merge_attention(0, 0, vx, a_cps[0])
    p_p = mlp(0, 0)
    merge_attention(0, 1, vx, a_cps[1])
    p_1 = mlp(0, 1)
    x_p = close_layer0(0, p_p)
    merge_attention(0, 2, vx, a_cps[2])
    p_2 = mlp(0, 2)
    own0 = wo_relay_own(1, 0, wo_y1[0])
    own1 = wo_relay_own(1, 1, wo_y1[1])
    for cp in w_qkv1:
        cp.wait()
    x_1 = close_layer0(1, p_1)
    x_p.wait_recv()
    project(1, 0, PIECE, rms(x1[0:PIECE].astype(F32), van[1:2, 0:D]), my_pos)
    kv_cps = share_kv(1)
    d0 = wo_relay_x(1, 0, own0[0])
    d1 = wo_relay_x(1, 1, own1[0])
    x_2 = close_layer0(2, p_2)

    x_1.wait_recv()
    project(1, 64, 128, rms(x1[64:192].astype(F32), van[1:2, 0:D]), PROMPT)
    for cp in kv_cps:
        cp.wait_recv()
    a_1 = attend(1, 1, PROMPT, 384)
    x_2.wait_recv()
    project(1, 192, 128, rms(x1[192:320].astype(F32), van[1:2, 0:D]), PROMPT + 128)
    a_2 = attend(1, 2, 384, 512)
    for cp in w_my1 + w_mlp1 + w_head:
        cp.wait()
    for cp in (own0[1], own1[1], d0, d1):
        cp.wait_recv()
    merge_attention(1, 1, x1, a_1)
    p_1 = mlp(1, 1)
    merge_attention(1, 2, x1, a_2)
    p_2 = mlp(1, 2)
    h_1 = close_layer1(1, p_1)
    h_2 = close_layer1(2, p_2)
    s_1 = head(1, h_1)
    s_2 = head(2, h_2)
    finish(1, s_1)
    finish(2, s_2)
    for cp in sent:
        cp.wait_send()


def solution(mesh):
    rows_spec = P(('prompts', 'resp'), None)
    in_specs = (rows_spec, P(('prompts', 'resp'), None, None), rows_spec, P(), P(),
                P(None, None, 'model', None), P(None, None, 'model', None), P(None, None, 'model', None),
                P(None, 'model', None, None), P(None, None, 'model'), P(None, None, 'model'),
                P(None, 'model', None), P(), P(None, 'model'))
    cos, sin = rope_constants()

    def local_pass(x_piece, x_own, tgt_own, attn_norm, mlp_norm, w_q, w_k, w_v, w_o, w_gate, w_up, w_down, final_norm, w_head):
        def rows_first(w):
            return jnp.transpose(w, (0, 2, 3, 1)).reshape(2, w.shape[2] * HD, D)

        any_spec = pl.BlockSpec(memory_space=pl.ANY)
        scratch = [
            pltpu.VMEM((ROWS, D), BF16), pltpu.VMEM((ROWS, 128), F32), pltpu.VMEM((ROWS, 128), F32), pltpu.VMEM((1, RESP), jnp.int32),
            pltpu.VMEM((2, GAIN_PAD), F32), pltpu.VMEM((2, GAIN_PAD), F32), pltpu.VMEM((1, GAIN_PAD), F32),
            pltpu.VMEM((2, 640, D), BF16), pltpu.VMEM((2, 512, D), BF16), pltpu.VMEM((2, 512, D), BF16),
            pltpu.VMEM((2, D, FF), BF16), pltpu.VMEM((2, D, FF), BF16), pltpu.VMEM((2, FF, D), BF16), pltpu.VMEM((D, VOC), BF16),
            pltpu.VMEM((2, PROMPT + RESP, 128), BF16), pltpu.VMEM((ROWS, 512), BF16), pltpu.VMEM((ROWS, 512), BF16),
            pltpu.VMEM((2, ROWS * 7 // 2, 128), BF16), pltpu.VMEM((2, ROWS * 7 // 2, 128), BF16),
            pltpu.VMEM((ROWS, D), BF16), pltpu.VMEM((128, FF), BF16),
            pltpu.VMEM((2, ROWS, D), F32), pltpu.VMEM((2, ROWS // 2, D), F32),
            pltpu.VMEM((ROWS, D), BF16), pltpu.VMEM((ROWS, D), BF16), pltpu.VMEM((128, VOC), F32),
            pltpu.VMEM((2, 8, 128), F32), pltpu.VMEM((2, 8, 128), F32),
            pltpu.SemaphoreType.DMA((48,)), pltpu.SemaphoreType.DMA((48,)), pltpu.SemaphoreType.DMA((48,)),
        ]
        return pl.pallas_call(
            kernel,
            out_shape=jax.ShapeDtypeStruct((1, RESP), F32),
            in_specs=[any_spec] * 16,
            out_specs=pl.BlockSpec(memory_space=pltpu.VMEM),
            scratch_shapes=scratch,
            compiler_params=pltpu.CompilerParams(collective_id=0, has_side_effects=True, vmem_limit_bytes=67043328),
        )(x_piece, x_own[0], tgt_own, attn_norm, mlp_norm, rows_first(w_q), rows_first(w_k), rows_first(w_v),
          w_o.reshape(2, QROWS, D), w_gate, w_up, w_down, final_norm[None, :], w_head, jnp.asarray(cos), jnp.asarray(sin))

    return jax.shard_map(local_pass, mesh=mesh, in_specs=in_specs, out_specs=rows_spec, check_vma=False)
```

time: 250 us -> 71.8 us (0.29)
  waiting for transfers between devices: 135 us -> 0 us
  Pallas kernels: 0 us -> 69.1 us
  matrix products: 49.2 us -> 0 us
  blocking collectives: 28.6 us -> 0 us
  between operations: 13.7 us -> 0.01 us
  other arithmetic: 13.3 us -> 0 us
  local copies, waits for them, and re-layouts: 9.75 us -> 2.5 us
    psum x4 -> x0, waiting for transfers between devices: 134 us -> none  [the longest x2 67.7 us: finish_layer(): lax.psum(jnp.dot(act_vals, w_down_l, preferred_element_type=jnp.float32),...]
    pallas_call x0 -> x1, Pallas kernels: none -> 69.1 us  [local_pass(): pl.pallas_call(kernel, out_shape=jax.ShapeDtypeStruct((1, RESP), F32), in...]
    dot_general x13 -> x0, matrix products: 47.2 us -> none  [the longest x2 17.2 us: finish_layer(): jnp.dot(act_vals, w_down_l, preferred_element_type=jnp.float32)]
    all_gather x2 -> x0, blocking collectives: 18.7 us -> none  [local_pass(): lax.all_gather(jnp.stack([k_tok[:piece_len], v_tok[:piece_len]]), 'resp',...]
    reduce_sum x8 -> x0, other arithmetic: 9.88 us -> none  [the longest x5 7.06 us: rms_norm(): mean_sq = jnp.mean(x_f * x_f, axis=-1, keepdims=True)]
    psum x1 -> x0, blocking collectives: 4.93 us -> none  [token_logp(): totals = lax.psum(jnp.stack([exp_sum, picked]), 'model')]
    pmax x1 -> x0, blocking collectives: 4.93 us -> none  [token_logp(): top_val = lax.pmax(jnp.max(logits, axis=-1), 'model')]
    unnamed x70 -> x1, local copies, waits for them, and re-layouts: 6.01 us -> 1.22 us
  transfers between devices with their start and end apart: 4 -> 0, of which waited for: 4 -> 0; matrix products, arithmetic and copies ran while one was open for 0% -> 0% of each run, Pallas kernels for 0% -> 0%
where the time goes in v1:
time: 71.8 us; the launch traced here: 71.6 us
  Pallas kernels  69.1 us (96%)
  local copies, waits for them, and re-layouts  2.5 us (3%)
    pallas_call x1, Pallas kernels, local_pass(): pl.pallas_call(kernel, out_shape=jax.ShapeDtypeStruct((1, RESP), F32), in...  69.1 us

profile of v1, /device:TPU:0, one launch (start us, length us, event | category | flops | bytes accessed | tf_op | source)
XLA Modules:
  0.0 71.6 jit_solution(13667721686322928018)
XLA Ops:
  0.0 1.3 %broadcast_in_dim.3.fn = f32[1,896]{1,0:T(1,128)} reshape(f32[896]{0:T(1024)} %param.28) | data formatting | bytes 7168 | tf_op jit(solution)/shard_map/broadcast_in_dim | solution.py:375
  1.3 69.1 %shard_map.154 = f32[1,256]{1,0:T(1,128)} custom-call(bf16[64,896]{1,0:T(8,128)(2,1)} %xp.1, bf16[256,896]{1,0:T(8,128)(2,1)} %bitcast.17, s32[1,256]{1,0:T(1,128)} %tgt.1, f32[2,896]{1,0:T(2,128)} %an.1, f32[2,896]{1,0:T(2,128)} %mn.1, bf16[2,448,896]{2,1,0:T(8,128)(2,1)} %bitcast.15, bf16[2,64,896]{2,1,0:T(8,128)(2,1)} %bitcast.18, ...), custom_call_target="tpu_custom_call" | custom-call | tf_op jit(solution)/shard_map/pallas_call | solution.py:367
  70.4 1.2 %copy.20 = f32[1,256]{1,0:T(1,128)} copy(f32[1,256]{1,0:T(1,128)} %shard_map.154) | data formatting | bytes 2048
